TPU v7x, 32 devices: a whole 2x2x4 slice. The times are simulated.
32 devices in a mesh: dp: 16 (over z, y, core), expert: 2 (over x).
Axes of the slice: x: 2, y: 2, z: 4, core: 2. Of those that a mesh axis runs over, the one named last changes fastest.
Arguments:
- tokens: bfloat16 [256, 6144], P(('dp', 'expert')), may hold values from -6 to 6
- router_now: float32 [6144, 8], P('dp'), may hold values from -0.078125 to 0.078125
- router_next: float32 [6144, 8], P('dp'), may hold values from -0.078125 to 0.078125
- w_gate: bfloat16 [8, 6144, 8192], P('expert', None, 'dp'), may hold values from -0.078125 to 0.078125
- w_up: bfloat16 [8, 6144, 8192], P('expert', None, 'dp'), may hold values from -0.078125 to 0.078125
- w_down: bfloat16 [8, 8192, 6144], P('expert', 'dp'), may hold values from -0.0625 to 0.0625
- expert_ids: int32 [256, 2], P(('dp', 'expert')), may hold values from 0 to 7, all different within a row; in each aligned block of 8 rows (0 to 7, 8 to 15, ...) at most 4 rows name the same one
- next_ids: int32 [256, 2], P(('dp', 'expert')), may hold values from 0 to 7, all different within a row
Outputs:
- layer_out: bfloat16 [256, 6144], P(('dp', 'expert'))
- next_logits: float32 [256, 8], P(('dp', 'expert'))
- next_weights: float32 [256, 2], P(('dp', 'expert'))
Inputs may be any that keep to these rules, and one draw needn't show every extreme that they name: `expert_ids`: each row names 2 different experts. Among the 8 rows of one device no expert is named by more than 4 rows, and on some devices one expert is named by exactly 4 rows. `next_ids`: each row names 2 different experts.
All inputs are finite; a program needn't handle non-finite values.
Results may differ from a plain program's by a relative error of at most 0.013.
Values may be sent and summed in bfloat16 or wider, within the bound.
A program may use at most 128 MiB of HBM per device.

v0:
```python
import functools

import jax
import jax.numpy as jnp
from jax import lax
from jax.experimental import pallas as pl
from jax.experimental.pallas import tpu as pltpu
from jax.sharding import PartitionSpec as P

epsilon = 1e-05
BOTH = ("dp", "expert")
ROOM = 1 << 21


def rms_normed(values):
    return values * lax.rsqrt(jnp.mean(values * values, axis=-1, keepdims=True) + epsilon)


def pair_weights(logits, chosen):
    picked = jnp.take_along_axis(logits, chosen, axis=1)
    first = jax.nn.sigmoid(picked[:, 0] - picked[:, 1])
    return jnp.stack([first, 1.0 - first], axis=1)


def ffn_kernel(
    in_slots, out_slots, columns, x_ref, share_ref, gate_hbm, up_hbm, down_hbm, out_ref,
    in_buf, down_buf, hidden, in_sem, down_sem,
):
    experts, width, units = gate_hbm.shape
    chunks = width // columns

    def in_copies(e):
        slot = lax.rem(e, in_slots)
        return [
            pltpu.make_async_copy(w.at[e], in_buf.at[slot, i], in_sem.at[slot, i])
            for i, w in enumerate((gate_hbm, up_hbm))
        ]

    def down_copy(n):
        slot = lax.rem(n, out_slots)
        at = pl.ds(pl.multiple_of(n * columns, 128), columns)
        return pltpu.make_async_copy(
            down_hbm.at[:, :, at], down_buf.at[slot], down_sem.at[slot]
        )

    for e in range(min(in_slots, experts)):
        for copy in in_copies(e):
            copy.start()
    for n in range(min(out_slots, chunks)):
        down_copy(n).start()

    def first(e, carry):
        slot = lax.rem(e, in_slots)
        gate_copy, up_copy = in_copies(e)
        gate_copy.wait()
        gate = jnp.dot(x_ref[...], in_buf[slot, 0], preferred_element_type=jnp.float32)
        up_copy.wait()
        upward = jnp.dot(x_ref[...], in_buf[slot, 1], preferred_element_type=jnp.float32)
        value = gate / (1.0 + jnp.exp(-gate)) * upward * share_ref[e]
        hidden[:, pl.ds(pl.multiple_of(e * units, 128), units)] = value.astype(jnp.bfloat16)

        @pl.when(e + in_slots < experts)
        def _():
            for copy in in_copies(e + in_slots):
                copy.start()

        return carry

    lax.fori_loop(0, experts, first, 0)

    def second(n, carry):
        slot = lax.rem(n, out_slots)
        down_copy(n).wait()
        weights = down_buf[slot].reshape(experts * units, columns)
        total = jnp.dot(hidden[...], weights, preferred_element_type=jnp.float32)
        out_ref[:, pl.ds(pl.multiple_of(n * columns, 128), columns)] = total.astype(jnp.bfloat16)

        @pl.when(n + out_slots < chunks)
        def _():
            down_copy(n + out_slots).start()

        return carry

    lax.fori_loop(0, chunks, second, 0)


def local_experts(everyone, share, w_gate, w_up, w_down):
    experts, width, units = w_gate.shape
    rows = everyone.shape[0]
    if rows * width > ROOM:
        total = jnp.zeros((rows, width), jnp.float32)
        for e in range(experts):
            gate = jnp.dot(everyone, w_gate[e], preferred_element_type=jnp.float32)
            upward = jnp.dot(everyone, w_up[e], preferred_element_type=jnp.float32)
            value = gate / (1.0 + jnp.exp(-gate)) * upward * share[e]
            value = value.astype(jnp.bfloat16)
            total = total + jnp.dot(value, w_down[e], preferred_element_type=jnp.float32)
        return total.astype(jnp.bfloat16)
    columns, in_slots, out_slots = 768, 3, 4
    vmem = pl.BlockSpec(memory_space=pltpu.VMEM)
    hbm = pl.BlockSpec(memory_space=pltpu.HBM)
    return pl.pallas_call(
        functools.partial(ffn_kernel, in_slots, out_slots, columns),
        out_shape=jax.ShapeDtypeStruct((rows, width), jnp.bfloat16),
        in_specs=[vmem, vmem, hbm, hbm, hbm],
        out_specs=vmem,
        scratch_shapes=[
            pltpu.VMEM((in_slots, 2, width, units), jnp.bfloat16),
            pltpu.VMEM((out_slots, experts, units, columns), jnp.bfloat16),
            pltpu.VMEM((rows, experts * units), jnp.bfloat16),
            pltpu.SemaphoreType.DMA((in_slots, 2)),
            pltpu.SemaphoreType.DMA((out_slots,)),
        ],
        compiler_params=pltpu.CompilerParams(vmem_limit_bytes=67043328),
        cost_estimate=pl.CostEstimate(
            flops=6 * rows * experts * width * units,
            bytes_accessed=6 * experts * width * units,
            transcendentals=0,
        ),
    )(everyone, share, w_gate, w_up, w_down)


def on_device(tokens, router_now, router_next, w_gate, w_up, w_down, expert_ids, next_ids):
    experts, width, units = w_gate.shape
    count = router_now.shape[1]
    resid = tokens.astype(jnp.float32)
    normed = rms_normed(resid)
    pair = lax.all_gather(normed.astype(jnp.bfloat16), "expert", axis=0, tiled=True)
    everyone = lax.all_gather(pair, "dp", axis=0, tiled=True)
    rows = everyone.shape[0]
    routers = jnp.concatenate([router_now.T, router_next.T], axis=0)
    routers = lax.all_gather(routers, "dp", axis=1, tiled=True)
    whole_now, whole_next = routers[:count], routers[count:]
    exact = functools.partial(
        lax.dot_general,
        dimension_numbers=(((1,), (1,)), ((), ())),
        precision=lax.Precision.HIGHEST,
        preferred_element_type=jnp.float32,
    )
    logits = exact(normed, whole_now)
    weights = pair_weights(logits, expert_ids)
    named = expert_ids[:, :, None] == jnp.arange(count, dtype=jnp.int32)[None, None, :]
    table = jnp.sum(jnp.where(named, weights[:, :, None], 0.0), axis=1)
    table = lax.all_gather(table, BOTH, axis=0, tiled=True)
    share = lax.dynamic_slice_in_dim(table, lax.axis_index("expert") * experts, experts, axis=1)
    share = share.T[:, :, None]

    partial = local_experts(everyone, share, w_gate, w_up, w_down)
    mixture = lax.psum_scatter(partial, "dp", scatter_dimension=0, tiled=True)
    mixture = lax.psum_scatter(mixture, "expert", scatter_dimension=0, tiled=True)
    summed = resid + mixture.astype(jnp.float32)
    layer_out = summed.astype(jnp.bfloat16)
    next_logits = exact(rms_normed(summed), whole_next)
    return (layer_out, next_logits, pair_weights(next_logits, next_ids))


def solution(mesh):
    in_specs = (
        P(BOTH, None),
        P("dp", None),
        P("dp", None),
        P("expert", None, "dp"),
        P("expert", None, "dp"),
        P("expert", "dp", None),
        P(BOTH, None),
        P(BOTH, None),
    )
    out_specs = (P(BOTH, None), P(BOTH, None), P(BOTH, None))
    return jax.shard_map(
        on_device, mesh=mesh, in_specs=in_specs, out_specs=out_specs, check_vma=False
    )
```

profile of v0, /device:TPU:0, one launch (start us, length us, event | category | flops | bytes accessed | tf_op | source)
XLA Modules:
  0.0 233.5 jit_solution(4848282449159048896)
XLA Ops:
  7.2 1.1 fusion.2
  8.3 1.0 fusion.1
  9.3 6.5 %all_gather.12 = bf16[16,6144]{1,0:T(8,128)(2,1)} all-gather(bf16[8,6144]{1,0:T(8,128)(2,1)S(1)} %fusion.1), channel_id=1, replica_groups=mesh['dp'=16,'expert'=2] {'expert'}, dimensions={0}, use_global_device_ids=true | all-gather | bytes 294912 | tf_op jit(solution)/shard_map/all_gather | solution.py:128
  15.9 0.8 copy.54
  16.6 0.1 copy.57
  16.7 0.1 copy.58
  16.8 0.1 reshape.56
  16.9 0.7 pad_maximum_fusion
  17.6 23.8 %all_gather.14 = f32[16,6144]{1,0:T(8,128)S(1)} all-gather(f32[16,384]{1,0:T(8,128)S(1)} %pad_maximum_fusion), channel_id=1, replica_groups=mesh['dp'=16,'expert'=2] {'dp'}, dimensions={1}, use_global_device_ids=true | all-gather | bytes 417792 | tf_op jit(solution)/shard_map/all_gather | solution.py:132
  41.4 0.7 copy-done.1
  42.2 1.5 fusion
  43.7 0.7 gather_fusion
  44.4 0.1 broadcast_subtract_fusion.1
  44.6 0.1 copy.59
  44.6 0.8 select_reduce_fusion
  45.4 65.9 %all_gather.15 = f32[256,8]{1,0:T(8,128)S(1)} all-gather(f32[8,8]{1,0:T(8,128)S(1)} %select_reduce_fusion), channel_id=1, replica_groups=mesh['dp'=16,'expert'=2] {'dp','expert'}, dimensions={0}, use_global_device_ids=true | all-gather | bytes 8448 | tf_op jit(solution)/shard_map/all_gather | solution.py:144
  111.3 0.1 dynamic-slice_bitcast_fusion
  111.4 2.7 %copy.61.share_ref = f32[4,256,1]{2,1,0:T(8,128)} copy(f32[4,256,1]{0,1,2:T(8,128)S(1)} %dynamic-slice_bitcast_fusion) | data formatting | bytes 8192 | tf_op jit(solution)/shard_map/broadcast_in_dim | solution.py:146
  114.1 32.7 %shard_map.103 = bf16[256,6144]{1,0:T(8,128)(2,1)} custom-call(bf16[256,6144]{1,0:T(8,128)(2,1)} %all-gather.2.cloned.1.call-done.x_ref, f32[4,256,1]{2,1,0:T(8,128)} %copy.61.share_ref, bf16[4,6144,512]{2,1,0:T(8,128)(2,1)} %gate_hbm.1, bf16[4,6144,512]{2,1,0:T(8,128)(2,1)} %up_hbm.1, bf16[4,512,6144]{2,1,0:T(8,128)(2,1)} %down_hbm.1), custom_call_target="tpu_custom_call" | custom-call | flops 19327352832 | bytes 75497472 | tf_op jit(solution)/shard_map/pallas_call | solution.py:102
  146.8 0.8 copy.62
  147.6 62.3 %reduce-scatter.3.cloned.1.call-done = bf16[16,6144]{1,0:T(8,128)(2,1)} async-done(((bf16[256,6144]{1,0:T(8,128)(2,1)}), bf16[16,6144]{1,0:T(8,128)(2,1)}) %reduce-scatter.3.cloned.1.call-update) | async-done | bytes 196624 | tf_op jit(solution)/shard_map/reduce_scatter | solution.py:149
  209.9 0.1 copy.65
  210.0 0.1 copy.66
  210.1 0.1 reshape.61
  210.2 11.8 %reduce-scatter.5.cloned.1.call-done = bf16[8,6144]{1,0:T(8,128)(2,1)} async-done(((bf16[16,6144]{1,0:T(8,128)(2,1)}), bf16[8,6144]{1,0:T(8,128)(2,1)}) %reduce-scatter.5.cloned.1.call-update) | async-done | bytes 98320 | tf_op jit(solution)/shard_map/reduce_scatter | solution.py:150
  222.0 1.7 multiply_reduce_fusion
  223.8 1.6 fusion.3
  225.4 0.7 gather_fusion.1
  226.1 0.1 broadcast_subtract_fusion
  226.2 0.1 copy.67
  226.3 0.1 copy.68
  226.4 0.6 pad_maximum_fusion.2
  (21 shorter events, 0.5 us)
Async XLA Ops:
  7.2 106.9 %all-gather.2.cloned.1.call-start = ((), (), s32[]{:S(2)}) async-start(), calls=%async_computation.2 | async-start | bytes 3342336 | tf_op jit(solution)/shard_map/all_gather | solution.py:129
  15.8 194.1 %reduce-scatter.3.cloned.1.call-start = ((), (), s32[]{:S(2)}) async-start(), calls=%async_computation.3 | async-start | bytes 3342336 | tf_op jit(solution)/shard_map/reduce_scatter | solution.py:149
  41.4 0.8 copy-start.1
  146.8 75.2 %reduce-scatter.5.cloned.1.call-start = ((), (), s32[]{:S(2)}) async-start(), calls=%async_computation.4 | async-start | bytes 294912 | tf_op jit(solution)/shard_map/reduce_scatter | solution.py:150
  225.4 1.6 copy-start
Sparse Core Ops, SparseCore 0:
  15.9 47.8 all-gather.1
  146.9 62.9 reduce-scatter.2
  212.1 9.8 reduce-scatter.4
where the time goes:
time: 234 us; the launch traced here: 233 us
  blocking collectives  96.2 us (41%)
  waiting for transfers between devices  74.2 us (32%)
  Pallas kernels  32.7 us (14%)
  between operations  13.8 us (6%)
  local copies, waits for them, and re-layouts  7.29 us (3%)
  other arithmetic  6.16 us (3%)
  matrix products  3.1 us (1%)
    all_gather x1, blocking collectives, on_device(): table = lax.all_gather(table, BOTH, axis=0, tiled=True)  65.9 us
    reduce_scatter x1, waiting for transfers between devices, on_device(): mixture = lax.psum_scatter(partial, 'dp', scatter_dimension=0, tiled=True)  62.3 us
    pallas_call x1, Pallas kernels, local_experts(): pl.pallas_call(functools.partial(ffn_kernel, in_slots, out_slots, columns...  32.7 us
    all_gather x1, blocking collectives, on_device(): routers = lax.all_gather(routers, 'dp', axis=1, tiled=True)  23.8 us
    reduce_scatter x1, waiting for transfers between devices, on_device(): lax.psum_scatter(mixture, 'expert', scatter_dimension=0, tiled=True)  11.8 us
    all_gather x1, blocking collectives, on_device(): lax.all_gather(normed.astype(jnp.bfloat16), 'expert', axis=0, tiled=True)  6.52 us
  transfers between devices with their start and end apart: 3, of which 2 were waited for; matrix products, arithmetic and copies ran while one was open for 4% of the time, Pallas kernels for 0%

commit v1 on v0

v1 whole, which is shorter than its diff:
```python
import functools

import jax
import jax.numpy as jnp
from jax import lax
from jax.experimental import pallas as pl
from jax.experimental.pallas import tpu as pltpu
from jax.sharding import PartitionSpec as P

epsilon = 1e-05
BOTH = ("dp", "expert")
ROOM = 1 << 21
CHUNKS = 4
POOL = 28
F32 = jnp.float32
BF16 = jnp.bfloat16


def rms_normed(values):
    return values * lax.rsqrt(jnp.mean(values * values, axis=-1, keepdims=True) + epsilon)


def pair_weights(logits, chosen):
    picked = jnp.take_along_axis(logits, chosen, axis=1)
    first = jax.nn.sigmoid(picked[:, 0] - picked[:, 1])
    return jnp.stack([first, 1.0 - first], axis=1)


def layer_kernel(
    depth,
    tokens_hbm, now_hbm, next_hbm, gate_hbm, up_hbm, down_hbm, ids_ref, next_ids_ref,
    out_ref, logits_ref, weights_ref,
    tok, now_own, now_low, now_all, next_own, next_all, xbuf, pool, acc, hidden,
    part, rd, ra, rb, rz, table,
    local_sem, in_sem, down_sem, small_send, small_recv,
    ag_send, ag_z, ag_pair, ag_core, rs_send, rs_core, rs_first, rs_second, rs_z,
):
    experts, width, units = gate_hbm.shape
    chunks, blocks, per, cols = xbuf.shape
    count = now_own.shape[0]
    mine = now_own.shape[1]
    rows = blocks * per
    groups = width // units
    per_chunk = cols // units
    pieces = chunks * experts * 2
    slots = pool.shape[0] // cols
    late = pieces - slots
    down_base = late * cols
    Z = depth

    d = lax.axis_index("dp")
    x = lax.axis_index("expert")
    core = lax.rem(d, 2)
    y = lax.rem(d // 2, 2)
    z = d // 4

    def peer(dk, dx, dy, dz):
        there = (lax.rem(z + dz, Z) * 2 + lax.rem(y + dy, 2)) * 2 + lax.rem(core + dk, 2)
        return {"dp": there, "expert": lax.rem(x + dx, 2)}

    def remote(src, dst, send, recv, to):
        return pltpu.make_async_remote_copy(
            src_ref=src, dst_ref=dst, send_sem=send, recv_sem=recv,
            device_id=to, device_id_type=pl.DeviceIdType.MESH,
        )

    near = peer(1, 0, 0, 0)

    def in_copy(p, g):
        chunk = p // (2 * experts)
        e = lax.rem(p // 2, experts)
        at = pl.multiple_of(lax.rem(p, slots) * cols, 512)
        source = (gate_hbm, up_hbm)[g].at[e, pl.ds(pl.multiple_of(chunk * cols, 512), cols), :]
        return pltpu.make_async_copy(source, pool.at[pl.ds(at, cols), :], in_sem.at[p])

    def down_copies(n):
        at = pl.ds(pl.multiple_of(n * units, 128), units)
        base = down_base + n * experts * units
        return [
            pltpu.make_async_copy(
                down_hbm.at[e, :, at],
                pool.at[pl.ds(pl.multiple_of(base + e * units, 512), units), :],
                down_sem.at[n, e],
            )
            for e in range(experts)
        ]

    small = [
        pltpu.make_async_copy(tokens_hbm, tok, local_sem.at[0]),
        pltpu.make_async_copy(now_hbm, now_own, local_sem.at[1]),
        pltpu.make_async_copy(next_hbm, next_own, local_sem.at[2]),
    ]
    for copy in small:
        copy.start()

    barrier = pltpu.get_barrier_semaphore()
    others = [
        (dk, dx, dy, dz)
        for dk in range(2) for dx in range(2) for dy in range(2) for dz in range(Z)
    ][1:]
    for to in others:
        pl.semaphore_signal(
            barrier, inc=1, device_id=peer(*to), device_id_type=pl.DeviceIdType.MESH
        )

    def begin(i, carry):
        for g in range(2):
            in_copy(i * 2 + g, g).start()
        return carry

    lax.fori_loop(0, slots // 2, begin, 0)

    small[0].wait()
    resid = tok[...].astype(F32)
    scale = lax.rsqrt(jnp.mean(resid * resid, axis=1, keepdims=True) + epsilon)
    rounded = (resid * scale).astype(BF16)
    for c in range(chunks):
        xbuf[c, 0] = rounded[:, c * cols:(c + 1) * cols]
    small[1].wait()
    own_at = pl.ds(pl.multiple_of(d * mine, 128), mine)
    now_low[...] = now_own[...].astype(BF16)
    now_all[:, own_at] = now_low[...]
    small[2].wait()
    next_all[:, own_at] = next_own[...]

    def clear(i, carry):
        acc[i] = jnp.zeros(acc.shape[1:], F32)
        return carry

    lax.fori_loop(0, acc.shape[0], clear, 0)
    pl.semaphore_wait(barrier, len(others))

    same_side = [to for to in others if to[1] == 0]

    def send_router(own, everyone, i):
        for to in same_side:
            remote(own, everyone.at[:, own_at], small_send.at[i], small_recv.at[i], peer(*to)).start()

    def router_bytes(everyone, i):
        span = everyone.at[:, pl.ds(0, mine * len(same_side))]
        return remote(span, span, small_send.at[i], small_recv.at[i], near)

    def choose(values, ids):
        eye = lax.broadcasted_iota(jnp.int32, (per, per), 0) == lax.broadcasted_iota(
            jnp.int32, (per, per), 1
        )
        names = [
            jnp.sum(jnp.where(eye, ids[i:i + 1, :].astype(F32), 0.0), axis=1, keepdims=True)
            for i in range(2)
        ]
        picked = [
            sum(jnp.where(name == float(e), values[e], 0.0) for e in range(count)) for name in names
        ]
        first = 1.0 / (1.0 + jnp.exp(picked[1] - picked[0]))
        return names, first

    def route():
        router_bytes(now_all, 0).wait_recv()
        whole = now_all[...].astype(F32)
        held = tok[...].astype(F32)
        values = [
            jnp.sum(held * whole[e:e + 1, :], axis=1, keepdims=True) * scale for e in range(count)
        ]
        names, first = choose(values, ids_ref[...])
        lane = lax.broadcasted_iota(jnp.int32, (per, 128), 1).astype(F32)
        table[0] = jnp.where(lane == names[0], first, 0.0) + jnp.where(
            lane == names[1], 1.0 - first, 0.0
        )
        for dk, dx, dy, dz in others:
            slot = ((dk * 2 + dx) * 2 + dy) * Z + (Z - dz) % Z
            remote(
                table.at[0], table.at[slot], small_send.at[1], small_recv.at[1], peer(dk, dx, dy, dz)
            ).start()

    def table_bytes():
        span = table.at[pl.ds(1, len(others))]
        return remote(span, span, small_send.at[1], small_recv.at[1], near)

    own_piece, rest_piece = (0, 1), (1, Z - 1)
    Y_LINE, X_LINE, FAR_LINE, CORE = Z, 2 * Z, 3 * Z, 4 * Z
    y_peer, x_peer = peer(0, 0, 1, 0), peer(0, 1, 0, 0)

    def lines(c):
        return ((Y_LINE, y_peer, X_LINE, x_peer) if c % 2 == 0 else (X_LINE, x_peer, Y_LINE, y_peer))

    def hop(c, which, part_index, source, target, to):
        start, size = (own_piece, rest_piece)[part_index]
        return remote(
            xbuf.at[c, pl.ds(source + start, size)], xbuf.at[c, pl.ds(target + start, size)],
            ag_send.at[c], ag_pair.at[c, which, part_index], to,
        )

    def across(c, i):
        return remote(
            xbuf.at[c, pl.ds(i * Z, Z)], xbuf.at[c, pl.ds(CORE + i * Z, Z)],
            ag_send.at[c], ag_core.at[c, i], near,
        )

    def gather_first(c):
        for dz in range(1, Z):
            remote(
                xbuf.at[c, 0], xbuf.at[c, Z - dz], ag_send.at[c], ag_z.at[c], peer(0, 0, 0, dz)
            ).start()
        a, a_peer, b, b_peer = lines(c)
        hop(c, 0, 0, 0, a, a_peer).start()
        hop(c, 1, 0, 0, b, b_peer).start()

    def gather_own(c):
        a, a_peer, b, b_peer = lines(c)
        hop(c, 0, 0, 0, a, a_peer).wait_recv()
        hop(c, 2, 0, a, FAR_LINE, b_peer).start()

    def gather_line(c):
        span = xbuf.at[c, pl.ds(1, Z - 1)]
        remote(span, span, ag_send.at[c], ag_z.at[c], near).wait_recv()
        a, a_peer, b, b_peer = lines(c)
        hop(c, 0, 1, 0, a, a_peer).start()
        hop(c, 1, 1, 0, b, b_peer).start()
        across(c, 0).start()

    def gather_far(c):
        a, a_peer, b, b_peer = lines(c)
        hop(c, 0, 1, 0, a, a_peer).wait_recv()
        hop(c, 2, 1, a, FAR_LINE, b_peer).start()
        across(c, a // Z).start()

    def gather_second(c):
        a, a_peer, b, b_peer = lines(c)
        for i in range(2):
            hop(c, 1, i, 0, b, b_peer).wait_recv()
        across(c, b // Z).start()

    def gather_last(c):
        a, a_peer, b, b_peer = lines(c)
        for i in range(2):
            hop(c, 2, i, a, FAR_LINE, b_peer).wait_recv()
        across(c, 3).start()

    def gather_done(c):
        for i in range(4):
            across(c, i).wait_recv()

    for c in range(chunks):
        gather_first(c)
    send_router(now_low, now_all, 0)
    for c in range(chunks):
        gather_own(c)
    gather_line(0)
    gather_line(1)
    route()
    gather_far(0)
    gather_line(2)
    gather_far(1)
    gather_second(0)
    gather_line(3)
    gather_last(0)

    hooks = {
        0: [(gather_done, 0), (gather_far, 2), (gather_second, 1)],
        1: [(gather_last, 1), (gather_far, 3)],
        2: [(gather_second, 2)],
        3: [(gather_last, 2)],
        4: [(gather_done, 1), (gather_second, 3)],
        5: [(gather_last, 3)],
        8: [(gather_done, 2)],
        12: [(gather_done, 3)],
    }

    def issue_after(s):
        due = []
        for n in range(groups):
            last = late + -(-((n + 1) * experts * units) // cols) - 1
            if last // 2 == s:
                due.append(n)
        return due

    def ahead(s, carry):
        for step, actions in hooks.items():
            @pl.when(s == step)
            def _(actions=actions):
                for action, c in actions:
                    action(c)

        @pl.when(s == 2 * experts)
        def _():
            send_router(next_own, next_all, 2)

        c = s // experts
        e = lax.rem(s, experts)
        inputs = xbuf[c].reshape(rows, cols)
        for g in range(2):
            p = s * 2 + g
            in_copy(p, g).wait()
            at = pl.multiple_of(lax.rem(p, slots) * cols, 512)
            value = jnp.dot(inputs, pool[pl.ds(at, cols), :], preferred_element_type=F32)
            acc[e * 2 + g] += value

        @pl.when(s < late // 2)
        def _():
            for g in range(2):
                in_copy(slots + s * 2 + g, g).start()

        for step in range(chunks * experts):
            due = issue_after(step)
            if due:
                @pl.when(s == step)
                def _(due=due):
                    for n in due:
                        for copy in down_copies(n):
                            copy.start()

        @pl.when(c == chunks - 1)
        def _():
            @pl.when(e == 0)
            def _():
                table_bytes().wait_recv()

            lane = lax.broadcasted_iota(jnp.int32, (rows, 128), 1)
            shares = table[...].reshape(rows, 128)
            share = jnp.sum(
                jnp.where(lane == x * experts + e, shares, 0.0), axis=1, keepdims=True
            )
            gate = acc[e * 2]
            value = gate / (1.0 + jnp.exp(-gate)) * acc[e * 2 + 1] * share
            hidden[:, pl.ds(pl.multiple_of(e * units, 128), units)] = value.astype(BF16)

        return carry

    lax.fori_loop(0, chunks * experts, ahead, 0)

    def scatter_core(c):
        return remote(
            part.at[c, pl.ds(CORE, CORE)], rd.at[c], rs_send.at[c], rs_core.at[c], near
        )

    def reverse(c):
        return ((X_LINE, x_peer, Y_LINE, y_peer) if c % 2 == 0 else (Y_LINE, y_peer, X_LINE, x_peer))

    def scatter_first(c, i):
        a, a_peer, b, b_peer = reverse(c)
        source = (a, FAR_LINE)[i]
        return remote(
            part.at[c, pl.ds(source, Z)], ra.at[c, i], rs_send.at[c], rs_first.at[c, i], a_peer
        )

    def scatter_second(c):
        a, a_peer, b, b_peer = reverse(c)
        return remote(
            part.at[c, pl.ds(b, Z)], rb.at[c], rs_send.at[c], rs_second.at[c], b_peer
        )

    def add_core(c):
        scatter_core(c).wait_recv()
        a, a_peer, b, b_peer = reverse(c)

        def add(at):
            span = pl.ds(at, Z)
            part[c, span] = (part[c, span].astype(F32) + rd[c, span].astype(F32)).astype(BF16)

        add(FAR_LINE)
        scatter_first(c, 1).start()
        add(a)
        scatter_first(c, 0).start()
        add(b)
        add(0)

    def add_first(c):
        a, a_peer, b, b_peer = reverse(c)
        scatter_first(c, 1).wait_recv()
        span = pl.ds(b, Z)
        part[c, span] = (part[c, span].astype(F32) + ra[c, 1].astype(F32)).astype(BF16)
        scatter_second(c).start()

    def add_second(c):
        scatter_first(c, 0).wait_recv()
        scatter_second(c).wait_recv()
        span = pl.ds(0, Z)
        part[c, span] = (
            part[c, span].astype(F32) + ra[c, 0].astype(F32) + rb[c].astype(F32)
        ).astype(BF16)
        for dz in range(1, Z):
            remote(
                part.at[c, dz], rz.at[c, Z - 1 - dz], rs_send.at[c], rs_z.at[c], peer(0, 0, 0, dz)
            ).start()

    def down(n, carry):
        c = n // per_chunk
        for copy in down_copies(n):
            copy.wait()
        at = pl.multiple_of(down_base + n * experts * units, 512)
        total = jnp.dot(
            hidden[...], pool[pl.ds(at, experts * units), :], preferred_element_type=F32
        )
        lanes = pl.ds(pl.multiple_of(lax.rem(n, per_chunk) * units, 128), units)
        part[c, :, :, lanes] = total.astype(BF16).reshape(blocks, per, units)
        for k in range(chunks):
            @pl.when(n == (k + 1) * per_chunk - 1)
            def _(k=k):
                scatter_core(k).start()
                if k:
                    add_core(k - 1)

        return carry

    lax.fori_loop(0, groups, down, 0)

    router_bytes(next_all, 2).wait_recv()
    held = {"square": jnp.zeros((per, 1), F32), "values": [jnp.zeros((per, 1), F32)] * count}

    def finish(c):
        span = rz.at[c]
        remote(span, span, rs_send.at[c], rs_z.at[c], near).wait_recv()
        at = slice(c * cols, (c + 1) * cols)
        mixture = part[c, 0].astype(F32)
        for i in range(Z - 1):
            mixture = mixture + rz[c, i].astype(F32)
        summed = tok[:, at].astype(F32) + mixture
        out_ref[:, at] = summed.astype(BF16)
        held["square"] = held["square"] + jnp.sum(summed * summed, axis=1, keepdims=True)
        held["values"] = [
            held["values"][e]
            + jnp.sum(summed * next_all[e:e + 1, at], axis=1, keepdims=True)
            for e in range(count)
        ]

    order = [(add_first, 0), (add_core, chunks - 1)]
    for c in range(1, chunks):
        order += [(add_first, c), (add_second, c - 1)]
    order.append((add_second, chunks - 1))
    for action, c in order:
        action(c)
    for c in range(chunks):
        finish(c)

    final = lax.rsqrt(held["square"] / float(width) + epsilon)
    values = [value * final for value in held["values"]]
    place = lax.broadcasted_iota(jnp.int32, (per, count), 1)
    logits_ref[...] = sum(jnp.where(place == e, values[e], 0.0) for e in range(count))
    names, first = choose(values, next_ids_ref[...])
    eye = lax.broadcasted_iota(jnp.int32, (per, per), 0) == lax.broadcasted_iota(
        jnp.int32, (per, per), 1
    )
    for i, value in enumerate((first, 1.0 - first)):
        weights_ref[i:i + 1, :] = jnp.sum(jnp.where(eye, value, 0.0), axis=0, keepdims=True)

    router_bytes(now_all, 0).wait_send()
    router_bytes(next_all, 2).wait_send()
    table_bytes().wait_send()
    for c in range(chunks):
        span = xbuf.at[c, pl.ds(1, blocks - 1)]
        remote(span, span, ag_send.at[c], ag_z.at[c], near).wait_send()
        span = part.at[c, pl.ds(1, blocks - 1)]
        remote(span, span, rs_send.at[c], rs_z.at[c], near).wait_send()


def fused_layer(
    dp, tokens, router_now, router_next, w_gate, w_up, w_down, expert_ids, next_ids
):
    experts, width, units = w_gate.shape
    per = tokens.shape[0]
    mine, count = router_now.shape
    depth = dp // 4
    blocks = dp * 2
    rows = blocks * per
    chunks, cols = CHUNKS, width // CHUNKS
    pieces = chunks * experts * 2
    groups = width // units
    vmem = pl.BlockSpec(memory_space=pltpu.VMEM)
    hbm = pl.BlockSpec(memory_space=pltpu.HBM)
    dma = pltpu.SemaphoreType.DMA
    layer_out, next_logits, next_weights = pl.pallas_call(
        functools.partial(layer_kernel, depth),
        out_shape=[
            jax.ShapeDtypeStruct((per, width), BF16),
            jax.ShapeDtypeStruct((per, count), F32),
            jax.ShapeDtypeStruct((2, per), F32),
        ],
        in_specs=[hbm] * 6 + [vmem] * 2,
        out_specs=[vmem] * 3,
        scratch_shapes=[
            pltpu.VMEM((per, width), BF16),
            pltpu.VMEM((count, mine), F32),
            pltpu.VMEM((count, mine), BF16),
            pltpu.VMEM((count, width), BF16),
            pltpu.VMEM((count, mine), F32),
            pltpu.VMEM((count, width), F32),
            pltpu.VMEM((chunks, blocks, per, cols), BF16),
            pltpu.VMEM((POOL * cols, units), BF16),
            pltpu.VMEM((experts * 2, rows, units), F32),
            pltpu.VMEM((rows, experts * units), BF16),
            pltpu.VMEM((chunks, blocks, per, cols), BF16),
            pltpu.VMEM((chunks, blocks // 2, per, cols), BF16),
            pltpu.VMEM((chunks, 2, depth, per, cols), BF16),
            pltpu.VMEM((chunks, depth, per, cols), BF16),
            pltpu.VMEM((chunks, depth - 1, per, cols), BF16),
            pltpu.VMEM((blocks, per, 128), F32),
            dma((3,)),
            dma((pieces,)),
            dma((groups, experts)),
            dma((3,)),
            dma((3,)),
            dma((chunks,)),
            dma((chunks,)),
            dma((chunks, 3, 2)),
            dma((chunks, 4)),
            dma((chunks,)),
            dma((chunks,)),
            dma((chunks, 2)),
            dma((chunks,)),
            dma((chunks,)),
        ],
        compiler_params=pltpu.CompilerParams(
            vmem_limit_bytes=67043328, collective_id=0, has_side_effects=True
        ),
    )(
        tokens, router_now.T, router_next.T, w_gate, w_up, w_down, expert_ids.T, next_ids.T
    )
    return layer_out, next_logits, next_weights.T


def gathered_layer(tokens, router_now, router_next, w_gate, w_up, w_down, expert_ids, next_ids):
    experts, width, units = w_gate.shape
    count = router_now.shape[1]
    resid = tokens.astype(F32)
    normed = rms_normed(resid)
    pair = lax.all_gather(normed.astype(BF16), "expert", axis=0, tiled=True)
    everyone = lax.all_gather(pair, "dp", axis=0, tiled=True)
    rows = everyone.shape[0]
    routers = jnp.concatenate([router_now.T, router_next.T], axis=0)
    routers = lax.all_gather(routers, "dp", axis=1, tiled=True)
    whole_now, whole_next = routers[:count], routers[count:]
    exact = functools.partial(
        lax.dot_general,
        dimension_numbers=(((1,), (1,)), ((), ())),
        precision=lax.Precision.HIGHEST,
        preferred_element_type=F32,
    )
    logits = exact(normed, whole_now)
    weights = pair_weights(logits, expert_ids)
    named = expert_ids[:, :, None] == jnp.arange(count, dtype=jnp.int32)[None, None, :]
    table = jnp.sum(jnp.where(named, weights[:, :, None], 0.0), axis=1)
    table = lax.all_gather(table, BOTH, axis=0, tiled=True)
    share = lax.dynamic_slice_in_dim(table, lax.axis_index("expert") * experts, experts, axis=1)
    share = share.T[:, :, None]
    total = jnp.zeros((rows, width), F32)
    for e in range(experts):
        gate = jnp.dot(everyone, w_gate[e], preferred_element_type=F32)
        upward = jnp.dot(everyone, w_up[e], preferred_element_type=F32)
        value = gate / (1.0 + jnp.exp(-gate)) * upward * share[e]
        total = total + jnp.dot(value.astype(BF16), w_down[e], preferred_element_type=F32)
    mixture = lax.psum_scatter(total.astype(BF16), "dp", scatter_dimension=0, tiled=True)
    mixture = lax.psum_scatter(mixture, "expert", scatter_dimension=0, tiled=True)
    summed = resid + mixture.astype(F32)
    next_logits = exact(rms_normed(summed), whole_next)
    return (summed.astype(BF16), next_logits, pair_weights(next_logits, next_ids))


def solution(mesh):
    dp, sides = mesh.shape["dp"], mesh.shape["expert"]

    def on_device(tokens, *rest):
        rows, width = tokens.shape[0] * dp * sides, tokens.shape[1]
        if sides == 2 and dp % 4 == 0 and rows * width <= ROOM:
            return fused_layer(dp, tokens, *rest)
        return gathered_layer(tokens, *rest)

    in_specs = (
        P(BOTH, None),
        P("dp", None),
        P("dp", None),
        P("expert", None, "dp"),
        P("expert", None, "dp"),
        P("expert", "dp", None),
        P(BOTH, None),
        P(BOTH, None),
    )
    out_specs = (P(BOTH, None), P(BOTH, None), P(BOTH, None))
    return jax.shard_map(
        on_device, mesh=mesh, in_specs=in_specs, out_specs=out_specs, check_vma=False
    )
```

time: 234 us -> 82.7 us (0.35)
  blocking collectives: 96.2 us -> 0 us
  waiting for transfers between devices: 74.2 us -> 0 us
  Pallas kernels: 32.7 us -> 77.8 us
  between operations: 13.8 us -> 0.64 us
  other arithmetic: 6.16 us -> 0 us
  local copies, waits for them, and re-layouts: 7.29 us -> 4.04 us
  matrix products: 3.1 us -> 0 us
    all_gather x3 -> x0, blocking collectives: 96.2 us -> none  [the longest x1 65.9 us: on_device(): table = lax.all_gather(table, BOTH, axis=0, tiled=True)]
    reduce_scatter x2 -> x0, waiting for transfers between devices: 74.1 us -> none  [the longest x1 62.3 us: on_device(): mixture = lax.psum_scatter(partial, 'dp', scatter_dimension=0, tiled=True)]
    pallas_call x1, Pallas kernels: 32.7 us -> 77.8 us  [fused_layer(): pl.pallas_call(functools.partial(layer_kernel, depth), out_shape=[jax.Sha...]
    reduce_sum x3 -> x0, other arithmetic: 3.55 us -> none  [the longest x2 2.78 us: rms_normed(): jnp.mean(values * values, axis=-1, keepdims=True) + epsilon]
    dot_general x2 -> x0, matrix products: 3.1 us -> none  [the longest x1 1.62 us: on_device(): next_logits = exact(rms_normed(summed), whole_next)]
    broadcast_in_dim x2 -> x0, local copies, waits for them, and re-layouts: 2.8 us -> none  [on_device(): share = share.T[:, :, None]]
  transfers between devices with their start and end apart: 3 -> 0, of which waited for: 2 -> 0; matrix products, arithmetic and copies ran while one was open for 4% -> 0% of each run, Pallas kernels for 0% -> 0%
where the time goes in v1:
time: 82.7 us; the launch traced here: 82.4 us
  Pallas kernels  77.8 us (94%)
  local copies, waits for them, and re-layouts  4.04 us (5%)
    pallas_call x1, Pallas kernels, fused_layer(): pl.pallas_call(functools.partial(layer_kernel, depth), out_shape=[jax.Sha...  77.8 us
    unnamed x3, local copies, waits for them, and re-layouts  4.04 us

profile of v1, /device:TPU:0, one launch (start us, length us, event | category | flops | bytes accessed | tf_op | source)
XLA Modules:
  0.0 82.4 jit_solution(18074561922038960671)
XLA Ops:
  0.6 77.8 %shard_map.103 = (bf16[8,6144]{1,0:T(8,128)(2,1)}, f32[8,8]{1,0:T(8,128)}, f32[2,8]{1,0:T(2,128)}) custom-call(bf16[8,6144]{1,0:T(8,128)(2,1)} %tokens_hbm.1, f32[8,384]{1,0:T(8,128)} %bitcast.5, f32[8,384]{1,0:T(8,128)} %bitcast.6, bf16[4,6144,512]{2,1,0:T(8,128)(2,1)} %gate_hbm.1, bf16[4,6144,512]{2,1,0:T(8,128)(2,1)} %up_hbm.1, ...), custom_call_target="tpu_custom_call" | custom-call | tf_op jit(solution)/shard_map/pallas_call | solution.py:471
  78.4 1.5 %copy.14 = bf16[8,6144]{1,0:T(8,128)(2,1)} copy(bf16[8,6144]{1,0:T(8,128)(2,1)} %get-tuple-element.12) | data formatting | bytes 196608
  79.9 1.3 %copy.15 = f32[8,8]{1,0:T(8,128)} copy(f32[8,8]{1,0:T(8,128)} %get-tuple-element.13) | data formatting | bytes 512
  81.2 1.2 %copy.16 = f32[8,2]{0,1:T(2,128)} copy(f32[8,2]{0,1:T(2,128)} %bitcast.9) | data formatting | bytes 128

commit v2 on v1

v2 whole, which is shorter than its diff:
```python
import functools

import jax
import jax.numpy as jnp
from jax import lax
from jax.experimental import pallas as pl
from jax.experimental.pallas import tpu as pltpu
from jax.sharding import PartitionSpec as P

epsilon = 1e-05
BOTH = ("dp", "expert")
ROOM = 1 << 21
SHARES = (4, 5, 7, 8)
POOL_ROWS = 18432
VMEM_LIMIT = 55000000
PAIR = 2
F32 = jnp.float32
BF16 = jnp.bfloat16


def rms_normed(values):
    return values * lax.rsqrt(jnp.mean(values * values, axis=-1, keepdims=True) + epsilon)


def pair_weights(logits, chosen):
    picked = jnp.take_along_axis(logits, chosen, axis=1)
    first = jax.nn.sigmoid(picked[:, 0] - picked[:, 1])
    return jnp.stack([first, 1.0 - first], axis=1)


def layer_kernel(
    depth, sizes,
    tok, now_own, next_own, gate_hbm, up_hbm, down_hbm, ids_ref, next_ids_ref,
    out_ref, logits_ref, weights_ref,
    now_low, now_all, next_all, xbuf, pool, acc, hidden,
    part, rd, ra, rb, rz, table,
    in_sem, down_sem, small_send, small_recv,
    ag_send, ag_z, ag_pair, ag_core, rs_send, rs_core, rs_first, rs_second, rs_z,
    own_first, own_second,
):
    experts, width, units = gate_hbm.shape
    blocks, per, _ = xbuf.shape
    chunks = len(sizes)
    starts = [sum(sizes[:c]) for c in range(chunks)]
    halves, _, _, _, wide = part.shape
    count = now_own.shape[0]
    mine = now_own.shape[1]
    rows = blocks * per
    groups = width // wide
    space = pool.shape[0]
    deep = experts * units
    Z = depth

    loads, place = [], 0
    for c in range(chunks):
        for e in range(experts):
            loads.append((place, sizes[c]))
            place += sizes[c]
    pieces = len(loads)
    down_base = place % space
    for n in range(groups):
        loads.append((place, deep))
        place += deep
    after = []
    for i, (start, size) in enumerate(loads):
        assert start // space == (start + size - 1) // space
        low, high = start - space, start + size - space
        held = [k for k in range(i) if loads[k][0] < high and sum(loads[k]) > low]
        after.append(max(held, default=-1))
    early = sum(1 for k in after[:pieces] if k < 0)
    assert max(after) < pieces

    d = lax.axis_index("dp")
    x = lax.axis_index("expert")
    core = lax.rem(d, 2)
    y = lax.rem(d // 2, 2)
    z = d // 4

    def peer(dk, dx, dy, dz):
        there = (lax.rem(z + dz, Z) * 2 + lax.rem(y + dy, 2)) * 2 + lax.rem(core + dk, 2)
        return {"dp": there, "expert": lax.rem(x + dx, 2)}

    def remote(src, dst, send, recv, to):
        return pltpu.make_async_remote_copy(
            src_ref=src, dst_ref=dst, send_sem=send, recv_sem=recv,
            device_id=to, device_id_type=pl.DeviceIdType.MESH,
        )

    near = peer(1, 0, 0, 0)

    def in_copies(c, e):
        at = lax.rem(loads[c * experts][0] + e * sizes[c], space)
        at = pl.ds(pl.multiple_of(at, 256), sizes[c])
        rows_at = pl.ds(starts[c], sizes[c])
        return [
            pltpu.make_async_copy(
                w.at[e, rows_at, :], pool.at[at, pl.ds(g * units, units)],
                in_sem.at[c * experts + e, g],
            )
            for g, w in enumerate((gate_hbm, up_hbm))
        ]

    def down_copies(n):
        at = pl.ds(pl.multiple_of(n * wide, 128), wide)
        base = lax.rem(down_base + n * deep, space)
        return [
            pltpu.make_async_copy(
                down_hbm.at[e, :, at],
                pool.at[pl.ds(pl.multiple_of(base + e * units, 512), units), :],
                down_sem.at[n, e],
            )
            for e in range(experts)
        ]

    barrier = pltpu.get_barrier_semaphore()
    others = [
        (dk, dx, dy, dz)
        for dk in range(2) for dx in range(2) for dy in range(2) for dz in range(Z)
    ][1:]
    for to in others:
        pl.semaphore_signal(
            barrier, inc=1, device_id=peer(*to), device_id_type=pl.DeviceIdType.MESH
        )

    for p in range(experts):
        for copy in in_copies(0, p):
            copy.start()

    resid = tok[...].astype(F32)
    scale = lax.rsqrt(jnp.mean(resid * resid, axis=1, keepdims=True) + epsilon)
    rounded = (resid * scale).astype(BF16)
    for c in range(chunks):
        xbuf[0, :, starts[c]:starts[c] + sizes[c]] = rounded[:, starts[c]:starts[c] + sizes[c]]
    own_at = pl.ds(pl.multiple_of(d * mine, 128), mine)
    now_low[...] = now_own[...].astype(BF16)
    pl.semaphore_wait(barrier, len(others))

    same_side = [to for to in others if to[1] == 0]

    def send_router(own, everyone, i):
        for to in same_side:
            remote(own, everyone.at[:, own_at], small_send.at[i], small_recv.at[i], peer(*to)).start()

    def router_bytes(everyone, i):
        span = everyone.at[:, pl.ds(0, mine * len(same_side))]
        return remote(span, span, small_send.at[i], small_recv.at[i], near)

    def choose(values, ids):
        eye = lax.broadcasted_iota(jnp.int32, (per, per), 0) == lax.broadcasted_iota(
            jnp.int32, (per, per), 1
        )
        names = [
            jnp.sum(jnp.where(eye, ids[i:i + 1, :].astype(F32), 0.0), axis=1, keepdims=True)
            for i in range(2)
        ]
        picked = [
            sum(jnp.where(name == float(e), values[e], 0.0) for e in range(count)) for name in names
        ]
        first = 1.0 / (1.0 + jnp.exp(picked[1] - picked[0]))
        return names, first

    def route(c):
        now_all[:, own_at] = now_low[...]
        router_bytes(now_all, 0).wait_recv()
        whole = now_all[...].astype(F32)
        held = tok[...].astype(F32)
        values = [
            jnp.sum(held * whole[e:e + 1, :], axis=1, keepdims=True) * scale for e in range(count)
        ]
        names, first = choose(values, ids_ref[...])
        lane = lax.broadcasted_iota(jnp.int32, (per, 128), 1).astype(F32)
        table[0] = jnp.where(lane == names[0], first, 0.0) + jnp.where(
            lane == names[1], 1.0 - first, 0.0
        )
        for dk, dx, dy, dz in others:
            slot = ((dk * 2 + dx) * 2 + dy) * Z + (Z - dz) % Z
            remote(
                table.at[0], table.at[slot], small_send.at[1], small_recv.at[1], peer(dk, dx, dy, dz)
            ).start()

    def table_bytes():
        span = table.at[pl.ds(1, len(others))]
        return remote(span, span, small_send.at[1], small_recv.at[1], near)

    own_piece, rest_piece = (0, 1), (1, Z - 1)
    Y_LINE, X_LINE, FAR_LINE, CORE = Z, 2 * Z, 3 * Z, 4 * Z
    y_peer, x_peer = peer(0, 0, 1, 0), peer(0, 1, 0, 0)

    def lines(c):
        return ((Y_LINE, y_peer, X_LINE, x_peer) if c % 2 == 0 else (X_LINE, x_peer, Y_LINE, y_peer))

    def piece(c, start, size):
        return xbuf.at[pl.ds(start, size), :, pl.ds(starts[c], sizes[c])]

    def hop(c, which, part_index, source, target, to):
        start, size = (own_piece, rest_piece)[part_index]
        return remote(
            piece(c, source + start, size), piece(c, target + start, size),
            ag_send.at[c], ag_pair.at[c, which, part_index], to,
        )

    def across(c, i):
        return remote(
            piece(c, i * Z, Z), piece(c, CORE + i * Z, Z),
            ag_send.at[c], ag_core.at[c, i], near,
        )

    def gather_first(c):
        a, a_peer, b, b_peer = lines(c)
        hop(c, 0, 0, 0, a, a_peer).start()
        hop(c, 1, 0, 0, b, b_peer).start()
        for dz in range(1, Z):
            remote(
                piece(c, 0, 1), piece(c, Z - dz, 1), ag_send.at[c], ag_z.at[c], peer(0, 0, 0, dz)
            ).start()

    def gather_own(c):
        a, a_peer, b, b_peer = lines(c)
        hop(c, 0, 0, 0, a, a_peer).wait_recv()
        hop(c, 2, 0, a, FAR_LINE, b_peer).start()

    def gather_line(c):
        span = piece(c, 1, Z - 1)
        remote(span, span, ag_send.at[c], ag_z.at[c], near).wait_recv()
        a, a_peer, b, b_peer = lines(c)
        hop(c, 0, 1, 0, a, a_peer).start()
        hop(c, 1, 1, 0, b, b_peer).start()
        across(c, 0).start()

    def gather_far(c):
        a, a_peer, b, b_peer = lines(c)
        hop(c, 0, 1, 0, a, a_peer).wait_recv()
        hop(c, 2, 1, a, FAR_LINE, b_peer).start()
        across(c, a // Z).start()

    def gather_second(c):
        a, a_peer, b, b_peer = lines(c)
        for i in range(2):
            hop(c, 1, i, 0, b, b_peer).wait_recv()
        across(c, b // Z).start()

    def gather_last(c):
        a, a_peer, b, b_peer = lines(c)
        for i in range(2):
            hop(c, 2, i, a, FAR_LINE, b_peer).wait_recv()
        across(c, 3).start()

    def gather_done(c):
        for i in range(4):
            across(c, i).wait_recv()

    for c in range(chunks):
        gather_first(c)
    send_router(now_low, now_all, 0)
    for p in range(experts, early):
        for copy in in_copies(p // experts, p % experts):
            copy.start()

    hooks = {
        -1: [
            (gather_own, 0), (gather_own, 1), (gather_line, 0), (gather_own, 2), (gather_own, 3),
            (gather_line, 1), (gather_far, 0), (gather_second, 0), (gather_line, 2),
            (gather_far, 1), (gather_second, 1), (gather_last, 0), (gather_line, 3),
        ],
        0: [(gather_done, 0)],
        2: [(gather_far, 2), (gather_second, 2), (gather_last, 1)],
        4: [(gather_done, 1), (gather_far, 3)],
        6: [(gather_last, 2), (gather_second, 3), (route, 0)],
        8: [(gather_done, 2)],
        10: [(gather_last, 3)],
        12: [(gather_done, 3)],
    }
    for action, c in hooks.pop(-1):
        action(c)

    freed = {}
    for i in range(early, len(loads)):
        freed.setdefault(max(after[i], 0), []).append(i)

    lane = lax.broadcasted_iota(jnp.int32, (rows, 128), 1)

    def ahead(c, i, carry):
        for step in range(c * experts, (c + 1) * experts, PAIR):
            if step in hooks:
                @pl.when(i * PAIR == step - c * experts)
                def _(actions=hooks[step]):
                    for action, at in actions:
                        action(at)

        for k in range(PAIR):
            for copy in in_copies(c, i * PAIR + k):
                copy.wait()
        for k in range(PAIR):
            e = i * PAIR + k
            at = lax.rem(loads[c * experts][0] + e * sizes[c], space)
            at = pl.ds(pl.multiple_of(at, 256), sizes[c])
            value = jnp.dot(
                xbuf[:, :, starts[c]:starts[c] + sizes[c]].reshape(rows, sizes[c]), pool[at, :],
                preferred_element_type=F32,
            )
            if c == 0:
                acc[e] = value
            elif c < chunks - 1:
                acc[e] += value
            else:
                value = value + acc[e]
                gate, upward = value[:, :units], value[:, units:]
                share = jnp.sum(
                    jnp.where(lane == x * experts + e, table[...].reshape(rows, 128), 0.0),
                    axis=1, keepdims=True,
                )
                value = gate / (1.0 + jnp.exp(-gate)) * upward * share
                hidden[:, pl.ds(pl.multiple_of(e * units, 128), units)] = value.astype(BF16)

        for first in range(c * experts, (c + 1) * experts, PAIR):
            steps = range(first, first + PAIR)
            if any(step in freed for step in steps):
                @pl.when(i * PAIR == first - c * experts)
                def _(steps=steps):
                    for step in steps:
                        for load in freed.get(step, []):
                            if load < pieces:
                                copies = in_copies(load // experts, load % experts)
                            else:
                                copies = down_copies(load - pieces)
                            for copy in copies:
                                copy.start()

        return carry

    for c in range(chunks):
        if c == 1:
            next_all[:, own_at] = next_own[...]
        if c == chunks - 1:
            send_router(next_own, next_all, 2)
            table_bytes().wait_recv()
        lax.fori_loop(0, experts // PAIR, functools.partial(ahead, c), 0)

    REST = pl.ds(1, Z - 1)

    def scatter_core(c):
        h, p = c // 2, c % 2
        return remote(
            part.at[h, p, pl.ds(CORE, CORE)], rd.at[h, p], rs_send.at[0], rs_core.at[h, p], near
        )

    def reverse(p):
        return ((X_LINE, x_peer, Y_LINE, y_peer) if p == 0 else (Y_LINE, y_peer, X_LINE, x_peer))

    def scatter_first(c, i):
        h, p = c // 2, c % 2
        a, a_peer, b, b_peer = reverse(p)
        source = (a, FAR_LINE)[i]
        return remote(
            part.at[h, p, pl.ds(source + 1, Z - 1)], ra.at[h, p, i, REST],
            rs_send.at[0], rs_first.at[h, p, i], a_peer,
        )

    def scatter_second(c):
        h, p = c // 2, c % 2
        a, a_peer, b, b_peer = reverse(p)
        return remote(
            part.at[h, p, pl.ds(b + 1, Z - 1)], rb.at[h, p, REST],
            rs_send.at[0], rs_second.at[h, p], b_peer,
        )

    def layer_first(p, i):
        a, a_peer, b, b_peer = reverse(p)
        source = (a, FAR_LINE)[i]
        return remote(
            part.at[:, p, source], ra.at[:, p, i, 0], rs_send.at[0], own_first.at[p, i], a_peer
        )

    def layer_second(p):
        a, a_peer, b, b_peer = reverse(p)
        return remote(
            part.at[:, p, b], rb.at[:, p, 0], rs_send.at[0], own_second.at[p], b_peer
        )

    def add_core(c):
        h, p = c // 2, c % 2
        scatter_core(c).wait_recv()
        a, a_peer, b, b_peer = reverse(p)

        def add(at):
            span = pl.ds(at, Z)
            part[h, p, span] = (
                part[h, p, span].astype(F32) + rd[h, p, span].astype(F32)
            ).astype(BF16)

        add(FAR_LINE)
        scatter_first(c, 1).start()
        add(a)
        scatter_first(c, 0).start()
        add(b)
        add(0)

    def add_first(c):
        h, p = c // 2, c % 2
        a, a_peer, b, b_peer = reverse(p)
        scatter_first(c, 1).wait_recv()
        span = pl.ds(b + 1, Z - 1)
        part[h, p, span] = (
            part[h, p, span].astype(F32) + ra[h, p, 1, REST].astype(F32)
        ).astype(BF16)
        scatter_second(c).start()

    def add_second(c):
        h, p = c // 2, c % 2
        scatter_first(c, 0).wait_recv()
        scatter_second(c).wait_recv()
        part[h, p, REST] = (
            part[h, p, REST].astype(F32)
            + ra[h, p, 0, REST].astype(F32) + rb[h, p, REST].astype(F32)
        ).astype(BF16)
        for dz in range(1, Z):
            remote(
                part.at[h, p, dz], rz.at[h, p, Z - 1 - dz],
                rs_send.at[0], rs_z.at[h, p], peer(0, 0, 0, dz),
            ).start()

    def layer_send(p):
        for i in (1, 0):
            layer_first(p, i).start()

    def layer_add(p):
        a, a_peer, b, b_peer = reverse(p)
        layer_first(p, 1).wait_recv()
        part[:, p, b] = (part[:, p, b].astype(F32) + ra[:, p, 1, 0].astype(F32)).astype(BF16)
        layer_second(p).start()

    def layer_wait(p):
        layer_first(p, 0).wait_recv()
        layer_second(p).wait_recv()

    ready = {groups - 3: (0,), groups - 2: (1,), groups - 1: (2,)}

    def down(n, carry):
        for copy in down_copies(n):
            copy.wait()
        at = pl.multiple_of(lax.rem(down_base + n * deep, space), 512)
        total = jnp.dot(
            hidden[...], pool[pl.ds(at, experts * units), :], preferred_element_type=F32
        )
        part[n // 2, lax.rem(n, 2)] = total.astype(BF16).reshape(blocks, per, wide)
        for k in range(groups):
            @pl.when(n == k)
            def _(k=k):
                scatter_core(k).start()
                if k:
                    add_core(k - 1)
                for c in ready.get(k, ()):
                    add_first(c)
                if k == groups - 1:
                    add_second(0)

        return carry

    lax.fori_loop(0, groups, down, 0)

    order = [(add_core, groups - 1)]
    for c in range(3, groups):
        if c == groups - 1:
            order += [(layer_send, 0), (layer_send, 1)]
        order += [(add_first, c), (add_second, c - 2)]
    order += [(add_second, groups - 2), (layer_add, 0), (add_second, groups - 1), (layer_add, 1)]
    for action, c in order:
        action(c)
    router_bytes(next_all, 2).wait_recv()

    held = {"square": jnp.zeros((per, 1), F32), "values": [jnp.zeros((per, 1), F32)] * count}

    def finish(c):
        h, p = c // 2, c % 2
        span = rz.at[h, p]
        remote(span, span, rs_send.at[0], rs_z.at[h, p], near).wait_recv()
        at = slice(c * wide, (c + 1) * wide)
        mixture = part[h, p, 0].astype(F32) + ra[h, p, 0, 0].astype(F32) + rb[h, p, 0].astype(F32)
        for i in range(Z - 1):
            mixture = mixture + rz[h, p, i].astype(F32)
        summed = tok[:, at].astype(F32) + mixture
        out_ref[:, at] = summed.astype(BF16)
        held["square"] = held["square"] + jnp.sum(summed * summed, axis=1, keepdims=True)
        held["values"] = [
            held["values"][e]
            + jnp.sum(summed * next_all[e:e + 1, at], axis=1, keepdims=True)
            for e in range(count)
        ]

    for p in range(2):
        layer_wait(p)
    for c in range(groups):
        finish(c)

    final = lax.rsqrt(held["square"] / float(width) + epsilon)
    values = [value * final for value in held["values"]]
    place = lax.broadcasted_iota(jnp.int32, (per, count), 1)
    logits_ref[...] = sum(jnp.where(place == e, values[e], 0.0) for e in range(count))
    names, first = choose(values, next_ids_ref[...])
    eye = lax.broadcasted_iota(jnp.int32, (per, per), 0) == lax.broadcasted_iota(
        jnp.int32, (per, per), 1
    )
    for i, value in enumerate((first, 1.0 - first)):
        weights_ref[i:i + 1, :] = jnp.sum(jnp.where(eye, value, 0.0), axis=0, keepdims=True)

    router_bytes(now_all, 0).wait_send()
    router_bytes(next_all, 2).wait_send()
    table_bytes().wait_send()
    for c in range(chunks):
        span = piece(c, 1, blocks - 1)
        remote(span, span, ag_send.at[c], ag_z.at[c], near).wait_send()
    span = part.at[:, :, pl.ds(1, blocks - 1)]
    remote(span, span, rs_send.at[0], rs_z.at[0, 0], near).wait_send()


def fused_layer(
    dp, tokens, router_now, router_next, w_gate, w_up, w_down, expert_ids, next_ids
):
    experts, width, units = w_gate.shape
    per = tokens.shape[0]
    mine, count = router_now.shape
    depth = dp // 4
    blocks = dp * 2
    rows = blocks * per
    sizes = tuple(width // sum(SHARES) * share for share in SHARES)
    chunks = len(sizes)
    wide = 2 * units
    pieces = chunks * experts
    groups = width // wide
    halves = groups // 2
    vmem = pl.BlockSpec(memory_space=pltpu.VMEM)
    hbm = pl.BlockSpec(memory_space=pltpu.HBM)
    dma = pltpu.SemaphoreType.DMA
    stay = functools.partial(pltpu.with_memory_space_constraint, memory_space=pltpu.HBM)
    layer_out, next_logits, next_weights = pl.pallas_call(
        functools.partial(layer_kernel, depth, sizes),
        out_shape=[
            jax.ShapeDtypeStruct((per, width), BF16),
            jax.ShapeDtypeStruct((per, count), F32),
            jax.ShapeDtypeStruct((2, per), F32),
        ],
        in_specs=[vmem] * 3 + [hbm] * 3 + [vmem] * 2,
        out_specs=[vmem] * 3,
        scratch_shapes=[
            pltpu.VMEM((count, mine), BF16),
            pltpu.VMEM((count, width), BF16),
            pltpu.VMEM((count, width), F32),
            pltpu.VMEM((blocks, per, width), BF16),
            pltpu.VMEM((POOL_ROWS, wide), BF16),
            pltpu.VMEM((experts, rows, wide), F32),
            pltpu.VMEM((rows, experts * units), BF16),
            pltpu.VMEM((halves, 2, blocks, per, wide), BF16),
            pltpu.VMEM((halves, 2, blocks // 2, per, wide), BF16),
            pltpu.VMEM((halves, 2, 2, depth, per, wide), BF16),
            pltpu.VMEM((halves, 2, depth, per, wide), BF16),
            pltpu.VMEM((halves, 2, depth - 1, per, wide), BF16),
            pltpu.VMEM((blocks, per, 128), F32),
            dma((pieces, 2)),
            dma((groups, experts)),
            dma((3,)),
            dma((3,)),
            dma((chunks,)),
            dma((chunks,)),
            dma((chunks, 3, 2)),
            dma((chunks, 4)),
            dma((1,)),
            dma((halves, 2)),
            dma((halves, 2, 2)),
            dma((halves, 2)),
            dma((halves, 2)),
            dma((2, 2)),
            dma((2,)),
        ],
        compiler_params=pltpu.CompilerParams(
            vmem_limit_bytes=VMEM_LIMIT, collective_id=0, has_side_effects=True
        ),
    )(
        *[stay(value) for value in (tokens, router_now.T, router_next.T)],
        w_gate, w_up, w_down, stay(expert_ids.T), stay(next_ids.T),
    )
    return layer_out, next_logits, next_weights.T


def gathered_layer(tokens, router_now, router_next, w_gate, w_up, w_down, expert_ids, next_ids):
    experts, width, units = w_gate.shape
    count = router_now.shape[1]
    resid = tokens.astype(F32)
    normed = rms_normed(resid)
    pair = lax.all_gather(normed.astype(BF16), "expert", axis=0, tiled=True)
    everyone = lax.all_gather(pair, "dp", axis=0, tiled=True)
    rows = everyone.shape[0]
    routers = jnp.concatenate([router_now.T, router_next.T], axis=0)
    routers = lax.all_gather(routers, "dp", axis=1, tiled=True)
    whole_now, whole_next = routers[:count], routers[count:]
    exact = functools.partial(
        lax.dot_general,
        dimension_numbers=(((1,), (1,)), ((), ())),
        precision=lax.Precision.HIGHEST,
        preferred_element_type=F32,
    )
    logits = exact(normed, whole_now)
    weights = pair_weights(logits, expert_ids)
    named = expert_ids[:, :, None] == jnp.arange(count, dtype=jnp.int32)[None, None, :]
    table = jnp.sum(jnp.where(named, weights[:, :, None], 0.0), axis=1)
    table = lax.all_gather(table, BOTH, axis=0, tiled=True)
    share = lax.dynamic_slice_in_dim(table, lax.axis_index("expert") * experts, experts, axis=1)
    share = share.T[:, :, None]
    total = jnp.zeros((rows, width), F32)
    for e in range(experts):
        gate = jnp.dot(everyone, w_gate[e], preferred_element_type=F32)
        upward = jnp.dot(everyone, w_up[e], preferred_element_type=F32)
        value = gate / (1.0 + jnp.exp(-gate)) * upward * share[e]
        total = total + jnp.dot(value.astype(BF16), w_down[e], preferred_element_type=F32)
    mixture = lax.psum_scatter(total.astype(BF16), "dp", scatter_dimension=0, tiled=True)
    mixture = lax.psum_scatter(mixture, "expert", scatter_dimension=0, tiled=True)
    summed = resid + mixture.astype(F32)
    next_logits = exact(rms_normed(summed), whole_next)
    return (summed.astype(BF16), next_logits, pair_weights(next_logits, next_ids))


def solution(mesh):
    dp, sides = mesh.shape["dp"], mesh.shape["expert"]

    def on_device(tokens, *rest):
        rows, width = tokens.shape[0] * dp * sides, tokens.shape[1]
        if sides == 2 and dp % 4 == 0 and rows * width <= ROOM:
            return fused_layer(dp, tokens, *rest)
        return gathered_layer(tokens, *rest)

    in_specs = (
        P(BOTH, None),
        P("dp", None),
        P("dp", None),
        P("expert", None, "dp"),
        P("expert", None, "dp"),
        P("expert", "dp", None),
        P(BOTH, None),
        P(BOTH, None),
    )
    out_specs = (P(BOTH, None), P(BOTH, None), P(BOTH, None))
    return jax.shard_map(
        on_device, mesh=mesh, in_specs=in_specs, out_specs=out_specs, check_vma=False
    )
```

time: 82.7 us -> 62.8 us (0.76)
  Pallas kernels: 77.8 us -> 60.2 us
  local copies, waits for them, and re-layouts: 4.04 us -> 1.8 us
    pallas_call x1, Pallas kernels: 77.8 us -> 60.2 us  [fused_layer(): pl.pallas_call(functools.partial(layer_kernel, depth, sizes), out_shape=[...]
    unnamed x3, local copies, waits for them, and re-layouts: 4.04 us -> 1.8 us
where the time goes in v2:
time: 62.8 us; the launch traced here: 62.7 us
  Pallas kernels  60.2 us (96%)
  local copies, waits for them, and re-layouts  1.8 us (3%)
  between operations  0.64 us (1%)
    pallas_call x1, Pallas kernels, fused_layer(): pl.pallas_call(functools.partial(layer_kernel, depth, sizes), out_shape=[...  60.2 us
    unnamed x3, local copies, waits for them, and re-layouts  1.8 us

profile of v2, /device:TPU:0, one launch (start us, length us, event | category | flops | bytes accessed | tf_op | source)
XLA Modules:
  0.0 62.7 jit_solution(2655226470038866143)
XLA Ops:
  0.6 60.2 %shard_map.103 = (bf16[8,6144]{1,0:T(8,128)(2,1)S(1)}, f32[8,8]{1,0:T(8,128)S(1)}, f32[2,8]{1,0:T(2,128)S(1)}) custom-call(bf16[8,6144]{1,0:T(8,128)(2,1)} %tok.1, f32[8,384]{1,0:T(8,128)} %bitcast.6, f32[8,384]{1,0:T(8,128)} %bitcast.7, bf16[4,6144,512]{2,1,0:T(8,128)(2,1)} %gate_hbm.1, bf16[4,6144,512]{2,1,0:T(8,128)(2,1)} %up_hbm.1, ...), custom_call_target="tpu_custom_call" | custom-call | tf_op jit(solution)/shard_map/pallas_call | solution.py:535
  60.9 0.6 %copy.14 = bf16[8,6144]{1,0:T(8,128)(2,1)} copy(bf16[8,6144]{1,0:T(8,128)(2,1)S(1)} %get-tuple-element.12) | data formatting | bytes 196608
  61.5 0.6 copy.15
  62.1 0.6 copy.16

commit v3 on v2

--- a/solution.py
+++ b/solution.py
@@ -30,11 +30,11 @@
 
 def layer_kernel(
     depth, sizes,
-    tok, now_own, next_own, gate_hbm, up_hbm, down_hbm, ids_ref, next_ids_ref,
+    tokens_hbm, now_hbm, next_hbm, gate_hbm, up_hbm, down_hbm, ids_hbm, next_ids_hbm,
     out_ref, logits_ref, weights_ref,
-    now_low, now_all, next_all, xbuf, pool, acc, hidden,
+    tok, now_own, next_own, ids_ref, next_ids_ref, now_low, now_all, next_all, xbuf, pool, acc, hidden,
     part, rd, ra, rb, rz, table,
-    in_sem, down_sem, small_send, small_recv,
+    local_sem, in_sem, down_sem, small_send, small_recv,
     ag_send, ag_z, ag_pair, ag_core, rs_send, rs_core, rs_first, rs_second, rs_z,
     own_first, own_second,
 ):
@@ -112,6 +112,14 @@
             for e in range(experts)
         ]
 
+    small = [
+        pltpu.make_async_copy(source, target, local_sem.at[i])
+        for i, (source, target) in enumerate((
+            (tokens_hbm, tok), (now_hbm, now_own), (next_hbm, next_own),
+            (ids_hbm, ids_ref), (next_ids_hbm, next_ids_ref),
+        ))
+    ]
+    small[0].start()
     barrier = pltpu.get_barrier_semaphore()
     others = [
         (dk, dx, dy, dz)
@@ -122,17 +130,19 @@
             barrier, inc=1, device_id=peer(*to), device_id_type=pl.DeviceIdType.MESH
         )
 
+    for copy in small[1:]:
+        copy.start()
     for p in range(experts):
         for copy in in_copies(0, p):
             copy.start()
 
+    small[0].wait()
     resid = tok[...].astype(F32)
     scale = lax.rsqrt(jnp.mean(resid * resid, axis=1, keepdims=True) + epsilon)
     rounded = (resid * scale).astype(BF16)
     for c in range(chunks):
         xbuf[0, :, starts[c]:starts[c] + sizes[c]] = rounded[:, starts[c]:starts[c] + sizes[c]]
     own_at = pl.ds(pl.multiple_of(d * mine, 128), mine)
-    now_low[...] = now_own[...].astype(BF16)
     pl.semaphore_wait(barrier, len(others))
 
     same_side = [to for to in others if to[1] == 0]
@@ -251,6 +261,9 @@
 
     for c in range(chunks):
         gather_first(c)
+    for copy in small[1:]:
+        copy.wait()
+    now_low[...] = now_own[...].astype(BF16)
     send_router(now_low, now_all, 0)
     for p in range(experts, early):
         for copy in in_copies(p // experts, p % experts):
@@ -259,14 +272,14 @@
     hooks = {
         -1: [
             (gather_own, 0), (gather_own, 1), (gather_line, 0), (gather_own, 2), (gather_own, 3),
-            (gather_line, 1), (gather_far, 0), (gather_second, 0), (gather_line, 2),
-            (gather_far, 1), (gather_second, 1), (gather_last, 0), (gather_line, 3),
+            (gather_line, 1), (gather_far, 0), (gather_second, 0), (gather_far, 1),
+            (gather_second, 1), (gather_line, 2), (gather_last, 0), (gather_line, 3),
         ],
         0: [(gather_done, 0)],
-        2: [(gather_far, 2), (gather_second, 2), (gather_last, 1)],
-        4: [(gather_done, 1), (gather_far, 3)],
-        6: [(gather_last, 2), (gather_second, 3), (route, 0)],
-        8: [(gather_done, 2)],
+        2: [(gather_last, 1)],
+        4: [(gather_far, 2), (gather_second, 2), (gather_done, 1)],
+        6: [(route, 0), (gather_far, 3)],
+        8: [(gather_last, 2), (gather_second, 3), (gather_done, 2)],
         10: [(gather_last, 3)],
         12: [(gather_done, 3)],
     }
@@ -458,16 +471,6 @@
 
     lax.fori_loop(0, groups, down, 0)
 
-    order = [(add_core, groups - 1)]
-    for c in range(3, groups):
-        if c == groups - 1:
-            order += [(layer_send, 0), (layer_send, 1)]
-        order += [(add_first, c), (add_second, c - 2)]
-    order += [(add_second, groups - 2), (layer_add, 0), (add_second, groups - 1), (layer_add, 1)]
-    for action, c in order:
-        action(c)
-    router_bytes(next_all, 2).wait_recv()
-
     held = {"square": jnp.zeros((per, 1), F32), "values": [jnp.zeros((per, 1), F32)] * count}
 
     def finish(c):
@@ -487,10 +490,20 @@
             for e in range(count)
         ]
 
-    for p in range(2):
-        layer_wait(p)
-    for c in range(groups):
-        finish(c)
+    def next_wait(i):
+        router_bytes(next_all, i).wait_recv()
+
+    last = groups - 1
+    order = [(add_core, last)]
+    for c in range(3, groups):
+        order += [(add_first, c), (add_second, c - 2)]
+    order[-1:-1] = [(layer_send, 0), (layer_send, 1)]
+    order += [(add_second, last - 1), (add_second, last), (layer_add, 0), (layer_add, 1)]
+    order += [(next_wait, 2), (layer_wait, 0)] + [(finish, c) for c in range(0, last - 1, 2)]
+    order += [(layer_wait, 1)] + [(finish, c) for c in range(1, last, 2)]
+    order += [(finish, last - 1), (finish, last)]
+    for action, c in order:
+        action(c)
 
     final = lax.rsqrt(held["square"] / float(width) + epsilon)
     values = [value * final for value in held["values"]]
@@ -539,9 +552,14 @@
             jax.ShapeDtypeStruct((per, count), F32),
             jax.ShapeDtypeStruct((2, per), F32),
         ],
-        in_specs=[vmem] * 3 + [hbm] * 3 + [vmem] * 2,
+        in_specs=[hbm] * 8,
         out_specs=[vmem] * 3,
         scratch_shapes=[
+            pltpu.VMEM((per, width), BF16),
+            pltpu.VMEM((count, mine), F32),
+            pltpu.VMEM((count, mine), F32),
+            pltpu.VMEM((2, per), jnp.int32),
+            pltpu.VMEM((2, per), jnp.int32),
             pltpu.VMEM((count, mine), BF16),
             pltpu.VMEM((count, width), BF16),
             pltpu.VMEM((count, width), F32),
@@ -555,6 +573,7 @@
             pltpu.VMEM((halves, 2, depth, per, wide), BF16),
             pltpu.VMEM((halves, 2, depth - 1, per, wide), BF16),
             pltpu.VMEM((blocks, per, 128), F32),
+            dma((5,)),
             dma((pieces, 2)),
             dma((groups, experts)),
             dma((3,)),

time: 62.8 us -> 61.3 us (0.976)
  Pallas kernels: 60.2 us -> 58.7 us
    pallas_call x1, Pallas kernels: 60.2 us -> 58.7 us  [fused_layer(): pl.pallas_call(functools.partial(layer_kernel, depth, sizes), out_shape=[...]
where the time goes in v3:
time: 61.3 us; the launch traced here: 61.1 us
  Pallas kernels  58.7 us (96%)
  local copies, waits for them, and re-layouts  1.8 us (3%)
  between operations  0.64 us (1%)
    pallas_call x1, Pallas kernels, fused_layer(): pl.pallas_call(functools.partial(layer_kernel, depth, sizes), out_shape=[...  58.7 us
    unnamed x3, local copies, waits for them, and re-layouts  1.8 us

profile of v3, /device:TPU:0, one launch (start us, length us, event | category | flops | bytes accessed | tf_op | source)
XLA Modules:
  0.0 61.1 jit_solution(3480585005413267546)
XLA Ops:
  0.6 58.7 %shard_map.103 = (bf16[8,6144]{1,0:T(8,128)(2,1)S(1)}, f32[8,8]{1,0:T(8,128)S(1)}, f32[2,8]{1,0:T(2,128)S(1)}) custom-call(bf16[8,6144]{1,0:T(8,128)(2,1)} %tokens_hbm.1, f32[8,384]{1,0:T(8,128)} %bitcast.6, f32[8,384]{1,0:T(8,128)} %bitcast.7, bf16[4,6144,512]{2,1,0:T(8,128)(2,1)} %gate_hbm.1, bf16[4,6144,512]{2,1,0:T(8,128)(2,1)} %up_hbm.1, ...), custom_call_target="tpu_custom_call" | custom-call | tf_op jit(solution)/shard_map/pallas_call | solution.py:548
  59.3 0.6 %copy.14 = bf16[8,6144]{1,0:T(8,128)(2,1)} copy(bf16[8,6144]{1,0:T(8,128)(2,1)S(1)} %get-tuple-element.12) | data formatting | bytes 196608
  60.0 0.6 copy.15
  60.5 0.6 copy.16

commit v4 on v3

--- a/solution.py
+++ b/solution.py
@@ -87,6 +87,7 @@
         )
 
     near = peer(1, 0, 0, 0)
+    far_first = sorted(range(1, Z), key=lambda dz: abs(2 * dz - Z))
 
     def in_copies(c, e):
         at = lax.rem(loads[c * experts][0] + e * sizes[c], space)
@@ -219,7 +220,7 @@
         a, a_peer, b, b_peer = lines(c)
         hop(c, 0, 0, 0, a, a_peer).start()
         hop(c, 1, 0, 0, b, b_peer).start()
-        for dz in range(1, Z):
+        for dz in far_first:
             remote(
                 piece(c, 0, 1), piece(c, Z - dz, 1), ag_send.at[c], ag_z.at[c], peer(0, 0, 0, dz)
             ).start()
@@ -426,7 +427,7 @@
             part[h, p, REST].astype(F32)
             + ra[h, p, 0, REST].astype(F32) + rb[h, p, REST].astype(F32)
         ).astype(BF16)
-        for dz in range(1, Z):
+        for dz in far_first:
             remote(
                 part.at[h, p, dz], rz.at[h, p, Z - 1 - dz],
                 rs_send.at[0], rs_z.at[h, p], peer(0, 0, 0, dz),

time: 61.3 us -> 61.6 us (level)
  no operation moved by 1% of the time
where the time goes in v4:
time: 61.6 us; the launch traced here: 61.5 us
  Pallas kernels  59 us (96%)
  local copies, waits for them, and re-layouts  1.8 us (3%)
  between operations  0.64 us (1%)
    pallas_call x1, Pallas kernels, fused_layer(): pl.pallas_call(functools.partial(layer_kernel, depth, sizes), out_shape=[...  59 us
    unnamed x3, local copies, waits for them, and re-layouts  1.8 us

profile of v4, /device:TPU:0, one launch (start us, length us, event | category | flops | bytes accessed | tf_op | source)
XLA Modules:
  0.0 61.5 jit_solution(9115367390088072367)
XLA Ops:
  0.6 59.0 %shard_map.103 = (bf16[8,6144]{1,0:T(8,128)(2,1)S(1)}, f32[8,8]{1,0:T(8,128)S(1)}, f32[2,8]{1,0:T(2,128)S(1)}) custom-call(bf16[8,6144]{1,0:T(8,128)(2,1)} %tokens_hbm.1, f32[8,384]{1,0:T(8,128)} %bitcast.6, f32[8,384]{1,0:T(8,128)} %bitcast.7, bf16[4,6144,512]{2,1,0:T(8,128)(2,1)} %gate_hbm.1, bf16[4,6144,512]{2,1,0:T(8,128)(2,1)} %up_hbm.1, ...), custom_call_target="tpu_custom_call" | custom-call | tf_op jit(solution)/shard_map/pallas_call | solution.py:549
  59.7 0.6 %copy.14 = bf16[8,6144]{1,0:T(8,128)(2,1)} copy(bf16[8,6144]{1,0:T(8,128)(2,1)S(1)} %get-tuple-element.12) | data formatting | bytes 196608
  60.3 0.6 copy.15
  60.9 0.6 copy.16
